TPU v7x, 32 devices: a whole 2x2x4 slice. The times are simulated.
32 devices in a mesh: replica: 16 (over z, x, core), spatial: 2 (over y).
Axes of the slice: x: 2, y: 2, z: 4, core: 2. Of those that a mesh axis runs over, the one named last changes fastest.
Arguments:
- grads: bfloat16 [16, 2, 852992], P('replica', 'spatial'), may hold values from -6 to 6
- master: float32 [852992], P(('replica', 'spatial')), may hold values from -0.06 to 0.06
- velocity: float32 [852992], P(('replica', 'spatial')), may hold values from -0.3 to 0.3
- layer_offsets: int32 [6], replicated, may hold values from 0 to 852736, as said below
- layer_sizes: int32 [6], replicated, may hold values from 256 to 589824
- lars_skip: int32 [6], replicated, may hold values from 0 to 1
Outputs:
- new_weights: bfloat16 [852992], replicated
- new_master: float32 [852992], P(('replica', 'spatial'))
- new_velocity: float32 [852992], P(('replica', 'spatial'))
Inputs may be any that keep to these rules, and one draw needn't show every extreme that they name: layer_offsets, layer_sizes and lars_skip describe the six tensors (a 256 x 1024 convolution, a 256 x 256 x 9 convolution, and two gains and two shifts of 256 entries) laid end to end in some order without gaps, the last of them always a gain or a shift; lars_skip is 1 exactly for the gains and shifts.
All inputs are finite; a program needn't handle non-finite values.
Results may differ from a plain program's by a relative error of at most 0.001.
Values may be sent and summed in bfloat16 or wider, within the bound.
A program may use at most 64 MiB of HBM per device.

v0:
```python
import jax
import jax.numpy as jnp
from jax import lax
from jax.sharding import PartitionSpec as P


def shards(grads, master, velocity, layer_offsets, layer_sizes, lars_skip):
    n_rep = lax.axis_size("replica")
    n_spa = lax.axis_size("spatial")
    shard = master.shape[0]
    position = lax.axis_index(("replica", "spatial")) * shard + jnp.arange(shard, dtype=jnp.int32)
    inside = (position[None, :] >= layer_offsets[:, None]) & (
        position[None, :] < (layer_offsets + layer_sizes)[:, None]
    )
    onehot = inside.astype(jnp.float32)
    received = lax.all_to_all(
        grads[0, 0].reshape(n_rep, n_spa * shard),
        "replica",
        split_axis=0,
        concat_axis=0,
        tiled=True,
    )
    first = jnp.sum(received.astype(jnp.float32), axis=0)
    summed = lax.psum_scatter(
        first.reshape(n_spa, shard), "spatial", scatter_dimension=0, tiled=True
    )
    grad = summed.reshape(shard) / (n_rep * n_spa)
    gsq_local = jnp.dot(onehot, grad * grad, precision=lax.Precision.HIGHEST)
    wsq_local = jnp.dot(onehot, master * master, precision=lax.Precision.HIGHEST)
    wsq, gsq = lax.psum((wsq_local, gsq_local), ("replica", "spatial"))
    wnorm = jnp.sqrt(wsq)
    gnorm = jnp.sqrt(gsq)
    skipped = lars_skip.astype(jnp.float32)
    ratio = 0.02 * wnorm / (gnorm + 0.001 * wnorm + 1e-06)
    trust = skipped + (1.0 - skipped) * ratio
    decay = (1.0 - skipped) * 0.001
    trust_pos = jnp.dot(trust, onehot, precision=lax.Precision.HIGHEST)
    decay_pos = jnp.dot(decay, onehot, precision=lax.Precision.HIGHEST)
    new_velocity = 0.9 * velocity + 8.0 * trust_pos * (grad + decay_pos * master)
    new_master = master - new_velocity
    new_weights = lax.all_gather(
        new_master.astype(jnp.bfloat16), ("replica", "spatial"), axis=0, tiled=True
    )
    return (new_weights, new_master, new_velocity)


def solution(mesh):
    return jax.shard_map(
        shards,
        mesh=mesh,
        in_specs=(
            P("replica", "spatial", None),
            P(("replica", "spatial")),
            P(("replica", "spatial")),
            P(),
            P(),
            P(),
        ),
        out_specs=(P(), P(("replica", "spatial")), P(("replica", "spatial"))),
        check_vma=False,
    )
```

profile of v0, /device:TPU:0, one launch (start us, length us, event | category | flops | bytes accessed | tf_op | source)
XLA Modules:
  0.0 341.0 jit_solution(4959349934665128111)
XLA Ops:
  7.2 37.8 %reduce.1 = bf16[852992]{0:T(1024)(128)(2,1)} reduce(bf16[1,1,852992]{2,1,0:T(2,128)(2,1)} %param.6, bf16[]{:T(256)} %constant.38), dimensions={0,1}, to_apply=%param.6.reduce_sub_computation | reduce | bytes 3411970 | tf_op args[0]
  44.9 3.0 all_to_all.8
  47.9 0.5 broadcast.54
  48.4 13.3 %reduce.8 = bf16[16,53312]{1,0:T(8,128)(2,1)} reduce(bf16[16,1,53312]{2,1,0:T(2,128)(2,1)S(1)} %all_to_all.8, bf16[]{:T(256)} %broadcast.54), dimensions={1}, to_apply=%all_to_all.8.reduce_sub_computation | reduce | bytes 3411970 | tf_op jit(solution)/shard_map/all_to_all | solution.py:16
  61.8 3.2 reshape.38
  65.0 0.0 copy-start.1
  65.0 0.0 copy-start.4
  65.0 0.0 copy-start.6
  65.0 0.0 copy-start.7
  65.0 7.6 %all-to-all-start = ((bf16[16,2,26656]{2,1,0:T(2,128)(2,1)}), bf16[16,2,26656]{2,1,0:T(2,128)(2,1)}, u32[]{:S(2)}, u32[]{:S(2)}) async-start(bf16[16,2,26656]{2,1,0:T(2,128)(2,1)} %reshape.38), calls=%async_computation | async-start | bytes 3424256 | tf_op jit(solution)/shard_map/all_to_all | solution.py:16
  72.5 0.0 all-reduce.8.cloned.1.call-start
  72.6 0.0 copy-done.1
  72.6 0.7 reshape.25
  73.4 0.0 copy-done.4
  73.4 0.0 copy-done.6
  73.4 0.0 copy-done.7
  73.4 0.7 dynamic-slice
  74.1 0.7 iota_add_fusion
  74.7 32.2 %all-to-all-done = bf16[16,2,26656]{2,1,0:T(2,128)(2,1)} async-done(((bf16[16,2,26656]{2,1,0:T(2,128)(2,1)}), bf16[16,2,26656]{2,1,0:T(2,128)(2,1)}, u32[]{:S(2)}, u32[]{:S(2)}) %all-to-all-start) | async-done | bytes 1706016 | tf_op jit(solution)/shard_map/all_to_all | solution.py:16
  106.9 10.5 %reshape.39 = bf16[16,1,53312]{2,1,0:T(2,128)(2,1)S(1)} reshape(bf16[16,2,26656]{2,1,0:T(2,128)(2,1)} %all-to-all-done) | data formatting | bytes 3411968
  117.4 0.0 copy-start.5
  117.4 5.2 %convert_reduce_fusion = f32[53312]{0:T(1024)} fusion(bf16[16,1,53312]{2,1,0:T(2,128)(2,1)S(1)} %reshape.39), kind=kLoop, calls=%fused_computation | loop fusion | flops 1652672 | bytes 1919232 | tf_op jit(solution)/shard_map/reduce_sum | solution.py:23
  122.6 0.0 copy-start.3
  122.6 1.8 reshape.22
  124.5 0.0 all-reduce.8.cloned.1.call-update
  124.5 0.0 all-reduce.6.cloned.1.call-start
  124.5 0.0 copy-done.5
  124.5 1.7 convolution_reduce_fusion
  126.2 0.0 copy-start.2
  126.3 2.1 convolution_bitcast_fusion.1
  128.3 24.0 %all-reduce.8.cloned.1.call-done = f32[2,26656]{1,0:T(2,128)} async-done(((f32[2,26656]{1,0:T(2,128)}), f32[2,26656]{1,0:T(2,128)}) %all-reduce.8.cloned.1.call-update) | async-done | bytes 213264
  152.3 2.0 fusion
  154.3 0.1 reshape.27
  154.4 0.0 copy-done.3
  154.4 1.1 convolution_bitcast_fusion
  155.5 39.4 %all-reduce.2 = (f32[6]{0:T(128)S(1)}, f32[6]{0:T(128)S(1)}) all-reduce(f32[6]{0:T(128)S(1)} %convolution_bitcast_fusion, f32[6]{0:T(128)S(1)} %convolution_bitcast_fusion.1), channel_id=1, replica_groups=mesh['replica'=16,'spatial'=2] {'replica','spatial'}, use_global_device_ids=true, to_apply=%region_3.0 | all-reduce | flops 12 | bytes 96 | tf_op jit(solution)/shard_map/psum | solution.py:30
  194.9 0.8 convolution_reduce_fusion.1
  195.8 0.0 copy-done.2
  195.8 0.7 fusion.22
  196.5 0.1 broadcast.25
  196.6 0.6 dynamic-update-slice
  197.2 0.0 copy-start
  197.2 1.2 copy-done
  198.4 0.0 all-reduce.6.cloned.1.call-update
  198.4 133.0 %all-reduce.6.cloned.1.call-done = bf16[852992]{0:T(1024)(128)(2,1)} async-done(((bf16[852992]{0:T(1024)(128)(2,1)}), bf16[852992]{0:T(1024)(128)(2,1)}) %all-reduce.6.cloned.1.call-update) | async-done | bytes 1706000
  331.5 2.7 copy.13
  (3 shorter events, 0.0 us)
Async XLA Ops:
  65.0 7.7 %copy-start.1 = (f32[26656]{0:T(1024)S(1)}, f32[26656]{0:T(1024)}, u32[]{:S(2)}) copy-start(f32[26656]{0:T(1024)} %param.7) | copy-start | bytes 319876
  65.0 8.4 %copy-start.4 = (s32[6]{0:T(128)S(1)}, s32[6]{0:T(128)}, u32[]{:S(2)}) copy-start(s32[6]{0:T(128)} %param.10) | copy-start | bytes 76
  65.0 8.4 %copy-start.6 = (s32[6]{0:T(128)S(1)}, s32[6]{0:T(128)}, u32[]{:S(2)}) copy-start(s32[6]{0:T(128)} %param.9) | copy-start | bytes 76
  65.0 8.4 %copy-start.7 = (u32[32]{0:T(128)S(1)}, u32[32]{0:T(128)}, u32[]{:S(2)}) copy-start(u32[32]{0:T(128)} %constant.36) | copy-start | bytes 388
  65.0 41.9 %all-to-all-start = ((bf16[16,2,26656]{2,1,0:T(2,128)(2,1)}), bf16[16,2,26656]{2,1,0:T(2,128)(2,1)}, u32[]{:S(2)}, u32[]{:S(2)}) async-start(bf16[16,2,26656]{2,1,0:T(2,128)(2,1)} %reshape.38), calls=%async_computation | async-start | bytes 3424256 | tf_op jit(solution)/shard_map/all_to_all | solution.py:16
  72.5 79.8 %all-reduce.8.cloned.1.call-start = ((), (), s32[]{:S(2)}) async-start(), calls=%async_computation.2 | async-start | bytes 428032
  117.4 7.1 %copy-start.5 = (s32[6]{0:T(128)S(1)}, s32[6]{0:T(128)}, u32[]{:S(2)}) copy-start(s32[6]{0:T(128)} %param.11) | copy-start | bytes 76
  122.6 31.8 %copy-start.3 = (s32[26656]{0:T(1024)S(1)}, s32[26656]{0:T(1024)}, u32[]{:S(2)}) copy-start(s32[26656]{0:T(1024)} %iota_add_fusion) | copy-start | bytes 319876
  124.5 207.0 %all-reduce.6.cloned.1.call-start = ((), (), s32[]{:S(2)}) async-start(), calls=%async_computation.1 | async-start | bytes 3411968
  126.2 69.5 %copy-start.2 = (f32[26656]{0:T(1024)S(1)}, f32[26656]{0:T(1024)}, u32[]{:S(2)}) copy-start(f32[26656]{0:T(1024)} %param.8) | copy-start | bytes 319876
  197.2 1.2 copy-start
Sparse Core Ops, SparseCore 0:
  124.6 27.6 all-reduce.7
  198.6 132.8 all-reduce.5
where the time goes:
time: 342 us; the launch traced here: 341 us
  waiting for transfers between devices  189 us (55%)
  other arithmetic  59.7 us (17%)
  blocking collectives  39.4 us (12%)
  local copies, waits for them, and re-layouts  25.2 us (7%)
  between operations  14.2 us (4%)
  starting transfers between devices  7.66 us (2%)
  matrix products  5.68 us (2%)
    unnamed x4, waiting for transfers between devices  157 us
    psum x1, blocking collectives, shards(): wsq, gsq = lax.psum((wsq_local, gsq_local), ('replica', 'spatial'))  39.4 us
    unnamed x1, other arithmetic  37.8 us
    all_to_all x1, waiting for transfers between devices, shards(): lax.all_to_all(grads[0, 0].reshape(n_rep, n_spa * shard), 'replica', spli...  32.2 us
    unnamed x22, local copies, waits for them, and re-layouts  19.1 us
    all_to_all x1, other arithmetic, shards(): lax.all_to_all(grads[0, 0].reshape(n_rep, n_spa * shard), 'replica', spli...  13.3 us
    all_to_all x1, starting transfers between devices, shards(): lax.all_to_all(grads[0, 0].reshape(n_rep, n_spa * shard), 'replica', spli...  7.57 us
  transfers between devices with their start and end apart: 3, of which 3 were waited for; matrix products, arithmetic and copies ran while one was open for 2% of the time, Pallas kernels for 0%

commit v1 on v0

--- a/solution.py
+++ b/solution.py
@@ -27,7 +27,7 @@
     grad = summed.reshape(shard) / (n_rep * n_spa)
     gsq_local = jnp.dot(onehot, grad * grad, precision=lax.Precision.HIGHEST)
     wsq_local = jnp.dot(onehot, master * master, precision=lax.Precision.HIGHEST)
-    wsq, gsq = lax.psum((wsq_local, gsq_local), ("replica", "spatial"))
+    wsq, gsq = lax.psum(lax.psum((wsq_local, gsq_local), "spatial"), "replica")
     wnorm = jnp.sqrt(wsq)
     gnorm = jnp.sqrt(gsq)
     skipped = lars_skip.astype(jnp.float32)

time: 342 us -> 335 us (0.980)
  waiting for transfers between devices: 189 us -> 185 us
    unnamed x4, waiting for transfers between devices: 157 us -> 153 us
    psum x1 -> x2, blocking collectives: 39.4 us -> 36.6 us  [shards(): wsq, gsq = lax.psum(lax.psum((wsq_local, gsq_local), 'spatial'), 'replica')]
where the time goes in v1:
time: 335 us; the launch traced here: 334 us
  waiting for transfers between devices  185 us (55%)
  other arithmetic  59.7 us (18%)
  blocking collectives  36.6 us (11%)
  local copies, waits for them, and re-layouts  25.2 us (8%)
  between operations  14.2 us (4%)
  starting transfers between devices  7.66 us (2%)
  matrix products  5.68 us (2%)
    unnamed x4, waiting for transfers between devices  153 us
    unnamed x1, other arithmetic  37.8 us
    psum x2, blocking collectives, shards(): wsq, gsq = lax.psum(lax.psum((wsq_local, gsq_local), 'spatial'), 'replica')  36.6 us
    all_to_all x1, waiting for transfers between devices, shards(): lax.all_to_all(grads[0, 0].reshape(n_rep, n_spa * shard), 'replica', spli...  32.2 us
    unnamed x22, local copies, waits for them, and re-layouts  19.1 us
    all_to_all x1, other arithmetic, shards(): lax.all_to_all(grads[0, 0].reshape(n_rep, n_spa * shard), 'replica', spli...  13.3 us
    all_to_all x1, starting transfers between devices, shards(): lax.all_to_all(grads[0, 0].reshape(n_rep, n_spa * shard), 'replica', spli...  7.57 us
  transfers between devices with their start and end apart: 3, of which 3 were waited for; matrix products, arithmetic and copies ran while one was open for 2% of the time, Pallas kernels for 0%

profile of v1, /device:TPU:0, one launch (start us, length us, event | category | flops | bytes accessed | tf_op | source)
XLA Modules:
  0.0 334.0 jit_solution(1149764006265285418)
XLA Ops:
  7.2 37.8 %reduce.1 = bf16[852992]{0:T(1024)(128)(2,1)} reduce(bf16[1,1,852992]{2,1,0:T(2,128)(2,1)} %param.6, bf16[]{:T(256)} %constant.38), dimensions={0,1}, to_apply=%param.6.reduce_sub_computation | reduce | bytes 3411970 | tf_op args[0]
  44.9 3.0 all_to_all.8
  47.9 0.5 broadcast.54
  48.4 13.3 %reduce.8 = bf16[16,53312]{1,0:T(8,128)(2,1)} reduce(bf16[16,1,53312]{2,1,0:T(2,128)(2,1)S(1)} %all_to_all.8, bf16[]{:T(256)} %broadcast.54), dimensions={1}, to_apply=%all_to_all.8.reduce_sub_computation | reduce | bytes 3411970 | tf_op jit(solution)/shard_map/all_to_all | solution.py:16
  61.8 3.2 reshape.38
  65.0 0.0 copy-start.1
  65.0 0.0 copy-start.4
  65.0 0.0 copy-start.6
  65.0 0.0 copy-start.7
  65.0 7.6 %all-to-all-start = ((bf16[16,2,26656]{2,1,0:T(2,128)(2,1)}), bf16[16,2,26656]{2,1,0:T(2,128)(2,1)}, u32[]{:S(2)}, u32[]{:S(2)}) async-start(bf16[16,2,26656]{2,1,0:T(2,128)(2,1)} %reshape.38), calls=%async_computation | async-start | bytes 3424256 | tf_op jit(solution)/shard_map/all_to_all | solution.py:16
  72.5 0.0 all-reduce.9.cloned.1.call-start
  72.6 0.0 copy-done.1
  72.6 0.7 reshape.25
  73.4 0.0 copy-done.4
  73.4 0.0 copy-done.6
  73.4 0.0 copy-done.7
  73.4 0.7 dynamic-slice
  74.1 0.7 iota_add_fusion
  74.7 32.2 %all-to-all-done = bf16[16,2,26656]{2,1,0:T(2,128)(2,1)} async-done(((bf16[16,2,26656]{2,1,0:T(2,128)(2,1)}), bf16[16,2,26656]{2,1,0:T(2,128)(2,1)}, u32[]{:S(2)}, u32[]{:S(2)}) %all-to-all-start) | async-done | bytes 1706016 | tf_op jit(solution)/shard_map/all_to_all | solution.py:16
  106.9 10.5 %reshape.39 = bf16[16,1,53312]{2,1,0:T(2,128)(2,1)S(1)} reshape(bf16[16,2,26656]{2,1,0:T(2,128)(2,1)} %all-to-all-done) | data formatting | bytes 3411968
  117.4 0.0 copy-start.5
  117.4 5.2 %convert_reduce_fusion = f32[53312]{0:T(1024)} fusion(bf16[16,1,53312]{2,1,0:T(2,128)(2,1)S(1)} %reshape.39), kind=kLoop, calls=%fused_computation | loop fusion | flops 1652672 | bytes 1919232 | tf_op jit(solution)/shard_map/reduce_sum | solution.py:23
  122.6 0.0 copy-start.3
  122.6 1.8 reshape.22
  124.5 0.0 all-reduce.9.cloned.1.call-update
  124.5 0.0 all-reduce.7.cloned.1.call-start
  124.5 0.0 copy-done.5
  124.5 1.7 convolution_reduce_fusion
  126.2 0.0 copy-start.2
  126.3 2.1 convolution_bitcast_fusion.1
  128.3 24.0 %all-reduce.9.cloned.1.call-done = f32[2,26656]{1,0:T(2,128)} async-done(((f32[2,26656]{1,0:T(2,128)}), f32[2,26656]{1,0:T(2,128)}) %all-reduce.9.cloned.1.call-update) | async-done | bytes 213264
  152.3 2.0 fusion
  154.3 0.1 reshape.27
  154.4 0.0 copy-done.3
  154.4 1.1 convolution_bitcast_fusion
  155.5 4.9 %all-reduce.3 = (f32[6]{0:T(128)S(1)}, f32[6]{0:T(128)S(1)}) all-reduce(f32[6]{0:T(128)S(1)} %convolution_bitcast_fusion, f32[6]{0:T(128)S(1)} %convolution_bitcast_fusion.1), channel_id=1, replica_groups=mesh['replica'=16,'spatial'=2] {'spatial'}, use_global_device_ids=true, to_apply=%region_4.0 | all-reduce | flops 12 | bytes 96 | tf_op jit(solution)/shard_map/psum | solution.py:30
  160.4 31.7 %all-reduce.2 = (f32[6]{0:T(128)S(1)}, f32[6]{0:T(128)S(1)}) all-reduce(f32[6]{0:T(128)S(1)} %get-tuple-element.5, f32[6]{0:T(128)S(1)} %get-tuple-element.6), channel_id=1, replica_groups=mesh['replica'=16,'spatial'=2] {'replica'}, use_global_device_ids=true, to_apply=%region_5.0 | all-reduce | flops 12 | bytes 96 | tf_op jit(solution)/shard_map/psum | solution.py:30
  192.1 0.8 convolution_reduce_fusion.1
  192.9 0.0 copy-done.2
  192.9 0.7 fusion.22
  193.7 0.1 broadcast.25
  193.8 0.6 dynamic-update-slice
  194.4 0.0 copy-start
  194.4 1.2 copy-done
  195.6 0.0 all-reduce.7.cloned.1.call-update
  195.6 128.8 %all-reduce.7.cloned.1.call-done = bf16[852992]{0:T(1024)(128)(2,1)} async-done(((bf16[852992]{0:T(1024)(128)(2,1)}), bf16[852992]{0:T(1024)(128)(2,1)}) %all-reduce.7.cloned.1.call-update) | async-done | bytes 1706000
  324.4 2.7 copy.13
  (3 shorter events, 0.0 us)
Async XLA Ops:
  65.0 7.7 %copy-start.1 = (f32[26656]{0:T(1024)S(1)}, f32[26656]{0:T(1024)}, u32[]{:S(2)}) copy-start(f32[26656]{0:T(1024)} %param.7) | copy-start | bytes 319876
  65.0 8.4 %copy-start.4 = (s32[6]{0:T(128)S(1)}, s32[6]{0:T(128)}, u32[]{:S(2)}) copy-start(s32[6]{0:T(128)} %param.10) | copy-start | bytes 76
  65.0 8.4 %copy-start.6 = (s32[6]{0:T(128)S(1)}, s32[6]{0:T(128)}, u32[]{:S(2)}) copy-start(s32[6]{0:T(128)} %param.9) | copy-start | bytes 76
  65.0 8.4 %copy-start.7 = (u32[32]{0:T(128)S(1)}, u32[32]{0:T(128)}, u32[]{:S(2)}) copy-start(u32[32]{0:T(128)} %constant.36) | copy-start | bytes 388
  65.0 41.9 %all-to-all-start = ((bf16[16,2,26656]{2,1,0:T(2,128)(2,1)}), bf16[16,2,26656]{2,1,0:T(2,128)(2,1)}, u32[]{:S(2)}, u32[]{:S(2)}) async-start(bf16[16,2,26656]{2,1,0:T(2,128)(2,1)} %reshape.38), calls=%async_computation | async-start | bytes 3424256 | tf_op jit(solution)/shard_map/all_to_all | solution.py:16
  72.5 79.8 %all-reduce.9.cloned.1.call-start = ((), (), s32[]{:S(2)}) async-start(), calls=%async_computation.2 | async-start | bytes 428032
  117.4 7.1 %copy-start.5 = (s32[6]{0:T(128)S(1)}, s32[6]{0:T(128)}, u32[]{:S(2)}) copy-start(s32[6]{0:T(128)} %param.11) | copy-start | bytes 76
  122.6 31.8 %copy-start.3 = (s32[26656]{0:T(1024)S(1)}, s32[26656]{0:T(1024)}, u32[]{:S(2)}) copy-start(s32[26656]{0:T(1024)} %iota_add_fusion) | copy-start | bytes 319876
  124.5 199.9 %all-reduce.7.cloned.1.call-start = ((), (), s32[]{:S(2)}) async-start(), calls=%async_computation.1 | async-start | bytes 3411968
  126.2 66.7 %copy-start.2 = (f32[26656]{0:T(1024)S(1)}, f32[26656]{0:T(1024)}, u32[]{:S(2)}) copy-start(f32[26656]{0:T(1024)} %param.8) | copy-start | bytes 319876
  194.4 1.2 copy-start
Sparse Core Ops, SparseCore 0:
  124.6 27.6 all-reduce.8
  195.7 128.6 all-reduce.6
